TPU v7x, 32 devices: a whole 2x2x4 slice. The times are simulated.
32 devices in a mesh: tm: 8 (over z, core), dp: 4 (over y, x).
Axes of the slice: x: 2, y: 2, z: 4, core: 2. Of those that a mesh axis runs over, the one named last changes fastest.
Arguments:
- encoded: bfloat16 [512, 80, 1024], P('dp', 'tm'), may hold values from -6 to 6
- queries: bfloat16 [512, 32, 1024], P(('dp', 'tm')), may hold values from -200 to 200
- cotangent: bfloat16 [512, 32, 1024], P(('dp', 'tm')), may hold values from -0.08886719 to 0.08886719
- lengths: int32 [512], P(('dp', 'tm')), may hold values from 2 to 80
- key_weight: bfloat16 [1024, 1024], replicated, may hold values from -0.1875 to 0.1875
- value_weight: bfloat16 [1024, 1024], replicated, may hold values from -0.1875 to 0.1875
Outputs:
- context: bfloat16 [512, 32, 1024], P(('dp', 'tm'))
- key_grad: float32 [1024, 1024], replicated
- value_grad: float32 [1024, 1024], replicated
Inputs may be any that keep to these rules, and one draw needn't show every extreme that they name: Sequence b attends only to source positions below lengths[b].
All inputs are finite; a program needn't handle non-finite values.
Results may differ from a plain program's by a relative error of at most 0.0069.
Values may be sent and summed in bfloat16 or wider, within the bound.
A program may use at most 128 MiB of HBM per device.

v0:
```python
import math

import jax
import jax.numpy as jnp
from jax import lax
from jax.sharding import PartitionSpec as P


def attend(queries, key_rows, value_rows, lengths, cotangent):
    score_scale = 1.0 / math.sqrt(queries.shape[-1])
    scores = (
        jnp.einsum("btd,bsd->bts", queries, key_rows, preferred_element_type=jnp.float32)
        * score_scale
    )
    positions = jnp.arange(key_rows.shape[1], dtype=jnp.int32)
    in_range = positions[None, None, :] < lengths[:, None, None]
    scores = jnp.where(in_range, scores, -1e30)
    row_max = jnp.max(scores, axis=-1, keepdims=True)
    weights = jnp.exp(scores - row_max)
    probabilities = weights / jnp.sum(weights, axis=-1, keepdims=True)
    probs_low = probabilities.astype(jnp.bfloat16)
    context = jnp.einsum(
        "bts,bsd->btd", probs_low, value_rows, preferred_element_type=jnp.float32
    ).astype(jnp.bfloat16)
    grad_probs = jnp.einsum(
        "btd,bsd->bts", cotangent, value_rows, preferred_element_type=jnp.float32
    )
    grad_scores = probabilities * (
        grad_probs - jnp.sum(probabilities * grad_probs, axis=-1, keepdims=True)
    )
    grad_low = grad_scores.astype(jnp.bfloat16)
    grad_values = jnp.einsum(
        "bts,btd->bsd", probs_low, cotangent, preferred_element_type=jnp.float32
    ).astype(jnp.bfloat16)
    grad_keys = (
        jnp.einsum("bts,btd->bsd", grad_low, queries, preferred_element_type=jnp.float32)
        * score_scale
    ).astype(jnp.bfloat16)
    return (context, grad_keys, grad_values)


def project(flattened, weight_matrix, shape):
    return (
        jnp.dot(flattened, weight_matrix, preferred_element_type=jnp.float32)
        .astype(jnp.bfloat16)
        .reshape(shape)
    )


def weight_term(flattened, gradient):
    model_width = flattened.shape[1]
    return lax.dot_general(
        flattened,
        gradient.reshape(-1, model_width),
        (((0,), (0,)), ((), ())),
        preferred_element_type=jnp.float32,
    )


def body(encoded, queries, cotangent, lengths, key_weight, value_weight):
    model_width = encoded.shape[2]
    regrouped = lax.all_to_all(encoded, "tm", split_axis=0, concat_axis=1, tiled=True)
    flattened = regrouped.reshape(-1, model_width)
    key_rows = project(flattened, key_weight, regrouped.shape)
    value_rows = project(flattened, value_weight, regrouped.shape)
    context, grad_keys, grad_values = attend(queries, key_rows, value_rows, lengths, cotangent)
    key_grad = weight_term(flattened, grad_keys)
    value_grad = weight_term(flattened, grad_values)
    key_grad, value_grad = lax.psum((key_grad, value_grad), ("tm", "dp"))
    return (context, key_grad, value_grad)


def solution(mesh):
    return jax.shard_map(
        body,
        mesh=mesh,
        in_specs=(
            P("dp", "tm", None),
            P(("dp", "tm"), None, None),
            P(("dp", "tm"), None, None),
            P(("dp", "tm")),
            P(),
            P(),
        ),
        out_specs=(P(("dp", "tm"), None, None), P(), P()),
        check_vma=False,
    )
```

profile of v0, /device:TPU:0, one launch (start us, length us, event | category | flops | bytes accessed | tf_op | source)
XLA Modules:
  0.0 355.5 jit_solution(7292842336370048144)
XLA Ops:
  7.2 0.0 copy-start
  7.2 5.5 %copy.14 = bf16[128,10,1024]{2,1,0:T(8,128)(2,1)} copy(bf16[128,10,1024]{2,0,1:T(8,128)(2,1)} %param.6) | data formatting | bytes 5242880 | tf_op args[0]
  12.7 6.5 %all-to-all-start = ((bf16[128,10,1024]{2,1,0:T(8,128)(2,1)}), bf16[128,10,1024]{2,1,0:T(8,128)(2,1)}, u32[]{:S(2)}, u32[]{:S(2)}) async-start(bf16[128,10,1024]{2,1,0:T(8,128)(2,1)} %copy.14), calls=%async_computation | async-start | bytes 8388608 | tf_op jit(solution)/shard_map/all_to_all | solution.py:62
  19.2 0.0 all-reduce.3.cloned.1.call-start
  19.2 0.0 copy-done.5
  19.3 0.1 iota_compare_fusion
  19.3 94.0 %all-to-all-done = bf16[128,10,1024]{2,1,0:T(8,128)(2,1)} async-done(((bf16[128,10,1024]{2,1,0:T(8,128)(2,1)}), bf16[128,10,1024]{2,1,0:T(8,128)(2,1)}, u32[]{:S(2)}, u32[]{:S(2)}) %all-to-all-start) | async-done | bytes 2621472 | tf_op jit(solution)/shard_map/all_to_all | solution.py:62
  113.3 5.0 %copy.19 = bf16[8,16,10,1024]{3,2,0,1:T(8,128)(2,1)} copy(bf16[8,16,10,1024]{3,2,1,0:T(8,128)(2,1)} %bitcast) | data formatting | bytes 5242880 | tf_op jit(solution)/shard_map/all_to_all | solution.py:62
  118.3 6.1 %reshape.46 = bf16[1280,1024]{1,0:T(8,128)(2,1)} reshape(bf16[16,8,10,1024]{3,2,1,0:T(8,128)(2,1)} %bitcast.35) | data formatting | bytes 5242880 | tf_op jit(solution)/shard_map/reshape | solution.py:63
  124.5 6.1 %convolution_convert_fusion = bf16[1280,1024]{1,0:T(8,128)(2,1)} fusion(bf16[1280,1024]{1,0:T(8,128)(2,1)} %reshape.46, bf16[1024,1024]{1,0:T(8,128)(2,1)S(1)} %copy-done), kind=kOutput, calls=%fused_computation.3 | convolution fusion | flops 2685665280 | bytes 7340032 | tf_op jit(solution)/shard_map/dot_general | solution.py:44
  130.6 0.0 copy-done.3
  130.6 3.1 convolution_convert_fusion.1
  133.7 0.8 fusion.4
  134.6 0.9 fusion.8
  135.4 4.6 %convolution_convert_fusion.2 = bf16[16,80,1024]{2,1,0:T(8,128)(2,1)} fusion(bf16[16,32,1024]{2,1,0:T(8,128)(2,1)} %param.8, f32[16,32]{1,0:T(8,128)S(1)} %get-tuple-element.14, f32[16,32,80]{2,1,0:T(8,128)S(1)} %fusion.4), kind=kOutput, calls=%fused_computation.7 | convolution fusion | flops 85320272 | bytes 3835904 | tf_op jit(solution)/shard_map/bts,btd->bsd/dot_general | solution.py:32
  140.0 3.6 %multiply_reduce_fusion = (f32[16,32]{1,0:T(8,128)S(1)}, f32[16,32,80]{2,1,0:T(8,128)}) fusion(f32[16,32,80]{2,1,0:T(8,128)} %get-tuple-element.15, f32[16,32]{1,0:T(8,128)S(1)} %get-tuple-element.14, bf16[16,80,1024]{2,1,0:T(8,128)(2,1)} %bitcast.36, bf16[16,32,1024]{2,1,0:T(8,128)(2,1)} %param.8), kind=kOutput, calls=%fused_computation.16 | convolution fusion | flops 84008448 | bytes 4001792 | tf_op jit(solution)/shard_map/btd,bsd->bts/dot_general | solution.py:25
  143.6 4.1 %multiply_convert_fusion = bf16[16,80,1024]{2,1,0:T(8,128)(2,1)} fusion(bf16[16,32,1024]{2,1,0:T(8,128)(2,1)S(1)} %copy-done.1, f32[16,32,80]{2,1,0:T(8,128)} %get-tuple-element.17, f32[16,32]{1,0:T(8,128)S(1)} %get-tuple-element.16, f32[16,32]{1,0:T(8,128)S(1)} %get-tuple-element.14, f32[16,32,80]{2,1,0:T(8,128)S(1)} %fusion.4), kind=kOutput, calls=%fused_computation.1 | convolution fusion | flops 86712912 | bytes 4001792 | tf_op jit(solution)/shard_map/bts,btd->bsd/dot_general | solution.py:36
  147.8 7.6 %convolution_bitcast_fusion.1 = f32[1024,1024]{0,1:T(8,128)} fusion(bf16[1280,1024]{1,0:T(8,128)(2,1)} %bitcast.40, bf16[1280,1024]{1,0:T(8,128)(2,1)} %reshape.46), kind=kOutput, calls=%fused_computation.6 | convolution fusion | flops 2684354560 | bytes 9437184 | tf_op jit(solution)/shard_map/dot_general | solution.py:52
  155.4 4.4 %convolution_bitcast_fusion = f32[1024,1024]{0,1:T(8,128)} fusion(bf16[1280,1024]{1,0:T(8,128)(2,1)S(1)} %bitcast.38, bf16[1280,1024]{1,0:T(8,128)(2,1)S(1)} %copy-done.4), kind=kOutput, calls=%fused_computation.5 | convolution fusion | flops 2684354560 | bytes 9437184 | tf_op jit(solution)/shard_map/dot_general | solution.py:52
  159.8 0.0 all-reduce.3.cloned.1.call-update
  159.9 3.8 %convolution_convert_fusion.3 = bf16[16,32,1024]{2,1,0:T(8,128)(2,1)} fusion(bf16[16,80,1024]{2,1,0:T(8,128)(2,1)} %bitcast.37, f32[16,32]{1,0:T(8,128)S(1)} %get-tuple-element.14, f32[16,32,80]{2,1,0:T(8,128)S(1)} %fusion.4), kind=kOutput, calls=%fused_computation.8 | convolution fusion | flops 84533840 | bytes 3835904 | tf_op jit(solution)/shard_map/bts,bsd->btd/dot_general | solution.py:22
  163.7 174.3 %all-reduce.3.cloned.1.call-done = (f32[1024,1024]{0,1:T(8,128)}, f32[1024,1024]{0,1:T(8,128)}) async-done(((f32[1024,1024]{0,1:T(8,128)}, f32[1024,1024]{0,1:T(8,128)}), (f32[1024,1024]{0,1:T(8,128)}, f32[1024,1024]{0,1:T(8,128)})) %all-reduce.3.cloned.1.call-update) | async-done | bytes 8388624 | tf_op jit(solution)/shard_map/psum | solution.py:69
  338.0 5.3 %copy.16 = f32[1024,1024]{1,0:T(8,128)} copy(f32[1024,1024]{0,1:T(8,128)} %get-tuple-element.12) | data formatting | bytes 8388608
  343.4 5.3 %copy.17 = f32[1024,1024]{1,0:T(8,128)} copy(f32[1024,1024]{0,1:T(8,128)} %get-tuple-element.13) | data formatting | bytes 8388608
  (11 shorter events, 0.0 us)
Async XLA Ops:
  7.2 117.3 %copy-start = (bf16[1024,1024]{1,0:T(8,128)(2,1)S(1)}, bf16[1024,1024]{1,0:T(8,128)(2,1)}, u32[]{:S(2)}) copy-start(bf16[1024,1024]{1,0:T(8,128)(2,1)} %param.11) | copy-start | bytes 6291460
  12.7 6.5 %copy-start.5 = (s32[16]{0:T(128)S(1)}, s32[16]{0:T(128)}, u32[]{:S(2)}) copy-start(s32[16]{0:T(128)} %param.9) | copy-start | bytes 196
  12.7 100.6 %all-to-all-start = ((bf16[128,10,1024]{2,1,0:T(8,128)(2,1)}), bf16[128,10,1024]{2,1,0:T(8,128)(2,1)}, u32[]{:S(2)}, u32[]{:S(2)}) async-start(bf16[128,10,1024]{2,1,0:T(8,128)(2,1)} %copy.14), calls=%async_computation | async-start | bytes 8388608 | tf_op jit(solution)/shard_map/all_to_all | solution.py:62
  19.2 318.8 %all-reduce.3.cloned.1.call-start = ((), (), s32[]{:S(2)}) async-start(), calls=%async_computation.1 | async-start | bytes 16777216 | tf_op jit(solution)/shard_map/psum | solution.py:69
  124.5 6.1 %copy-start.3 = (bf16[1280,1024]{1,0:T(8,128)(2,1)S(1)}, bf16[1280,1024]{1,0:T(8,128)(2,1)}, u32[]{:S(2)}) copy-start(bf16[1280,1024]{1,0:T(8,128)(2,1)} %reshape.46) | copy-start | bytes 7864324
  124.5 6.1 %copy-start.6 = (bf16[1024,1024]{1,0:T(8,128)(2,1)S(1)}, bf16[1024,1024]{1,0:T(8,128)(2,1)}, u32[]{:S(2)}) copy-start(bf16[1024,1024]{1,0:T(8,128)(2,1)} %param.10) | copy-start | bytes 6291460
  130.6 3.1 copy-start.1
  147.8 7.6 %copy-start.2 = (bf16[16,80,1024]{2,1,0:T(8,128)(2,1)S(1)}, bf16[16,80,1024]{2,1,0:T(8,128)(2,1)}, u32[]{:S(2)}) copy-start(bf16[16,80,1024]{2,1,0:T(8,128)(2,1)} %convolution_convert_fusion.2) | copy-start | bytes 7864324
  147.8 7.6 %copy-start.4 = (bf16[1280,1024]{1,0:T(8,128)(2,1)S(1)}, bf16[1280,1024]{1,0:T(8,128)(2,1)}, u32[]{:S(2)}) copy-start(bf16[1280,1024]{1,0:T(8,128)(2,1)} %reshape.46) | copy-start | bytes 7864324
Sparse Core Ops, SparseCore 0:
  160.0 177.9 all-reduce.2
where the time goes:
time: 356 us
  waiting for transfers between devices  268 us (75%)
  matrix products  38.3 us (11%)
  local copies, waits for them, and re-layouts  27.4 us (8%)
  between operations  14.1 us (4%)
  starting transfers between devices  6.52 us (2%)
    psum x1, waiting for transfers between devices, body(): key_grad, value_grad = lax.psum((key_grad, value_grad), ('tm', 'dp'))  174 us
    all_to_all x1, waiting for transfers between devices, body(): lax.all_to_all(encoded, 'tm', split_axis=0, concat_axis=1, tiled=True)  94 us
    unnamed x17, local copies, waits for them, and re-layouts  16.2 us
    dot_general x2, matrix products, weight_term(): lax.dot_general(flattened, gradient.reshape(-1, model_width), (((0,), (0,...  12.1 us
    dot_general x2, matrix products, project(): jnp.dot(flattened, weight_matrix, preferred_element_type=jnp.float32)  9.23 us
  transfers between devices with their start and end apart: 2, of which 2 were waited for; matrix products, arithmetic and copies ran while one was open for 1% of the time, Pallas kernels for 0%

commit v1 on v0

v1 whole, which is shorter than its diff:
```python
import functools
import math

import jax
import jax.numpy as jnp
from jax import lax
from jax.experimental import pallas as pl
from jax.experimental.pallas import tpu as pltpu
from jax.sharding import PartitionSpec as P

MESH = pl.DeviceIdType.MESH


def bit_of(index, k):
    return lax.rem(index // (1 << k), 2)


def flip(index, mask):
    k = 0
    while (1 << k) <= mask:
        if mask & (1 << k):
            index = index + (1 - 2 * bit_of(index, k)) * (1 << k)
        k += 1
    return index


def greet(devices):
    barrier = pltpu.get_barrier_semaphore()
    for device in devices:
        pl.semaphore_signal(barrier, inc=1, device_id=device, device_id_type=MESH)
    pl.semaphore_wait(barrier, len(devices))


def exchange_kernel(n, enc_ref, out_ref, send_sem, recv_sem, own_sem):
    me = lax.axis_index("tm")
    seqs = out_ref.shape[2]
    greet([{"tm": flip(me, d)} for d in range(1, n)])
    copies = []
    for d in range(n - 1, 0, -1):
        target = flip(me, d)
        copy = pltpu.make_async_remote_copy(
            src_ref=enc_ref.at[:, pl.ds(pl.multiple_of(target * seqs, seqs), seqs), :],
            dst_ref=out_ref.at[me],
            send_sem=send_sem.at[d],
            recv_sem=recv_sem.at[d],
            device_id={"tm": target},
            device_id_type=MESH,
        )
        copy.start()
        copies.append(copy)
    own = pltpu.make_async_copy(
        enc_ref.at[:, pl.ds(pl.multiple_of(me * seqs, seqs), seqs), :], out_ref.at[me], own_sem
    )
    own.start()
    own.wait()
    for copy in copies:
        copy.wait()


def exchange(encoded, n):
    by_position = jnp.swapaxes(encoded, 0, 1)
    positions, rows, width = by_position.shape
    return pl.pallas_call(
        functools.partial(exchange_kernel, n),
        out_shape=jax.ShapeDtypeStruct((n, positions, rows // n, width), encoded.dtype),
        in_specs=[pl.BlockSpec(memory_space=pltpu.VMEM)],
        out_specs=pl.BlockSpec(memory_space=pltpu.VMEM),
        scratch_shapes=[
            pltpu.SemaphoreType.DMA((n,)),
            pltpu.SemaphoreType.DMA((n,)),
            pltpu.SemaphoreType.DMA,
        ],
        compiler_params=pltpu.CompilerParams(
            collective_id=0, has_side_effects=True, vmem_limit_bytes=40 << 20
        ),
    )(by_position)


def orders_of(bits_tm, bits_dp):
    middle = [("dp", k) for k in range(bits_dp)] + [("tm", k) for k in range(1, bits_tm - 1)]
    last = [("tm", bits_tm - 1)] if bits_tm > 1 else []
    return [middle[p:] + middle[:p] + last for p in range(3)]


def partner_of(position, step):
    axis, k = step
    return {axis: flip(position[axis], 1 << k)}


def sum_kernel(bits, key_ref, value_ref, out_ref, held, staged, landed, send_sem, recv_sem):
    position = {"tm": lax.axis_index("tm"), "dp": lax.axis_index("dp")}
    rows, width = key_ref.shape
    orders = orders_of(*bits)
    tiles = width // 128
    edges = [0, (tiles * 3 // 8) * 128, (tiles * 6 // 8) * 128, width]
    greet(
        [partner_of(position, ("tm", k)) for k in range(bits[0])]
        + [partner_of(position, ("dp", k)) for k in range(bits[1])]
    )
    core = bit_of(position["tm"], 0)
    chunk = 64

    def each(start, size, body):
        piece = min(chunk, size)

        @pl.loop(0, size // piece)
        def _(i):
            body(pl.ds(pl.multiple_of(start + i * piece, piece), piece), i * piece, piece)

    def send(src, dst, slot, device):
        copy = pltpu.make_async_remote_copy(
            src_ref=src,
            dst_ref=dst,
            send_sem=send_sem.at[slot],
            recv_sem=recv_sem.at[slot],
            device_id=device,
            device_id_type=MESH,
        )
        copy.start()
        return copy

    def stage_core(ref):
        def body(at, _, __):
            staged[at, :] = ref[at, :].astype(staged.dtype)

        each(0, rows, body)

    @pl.when(core == 0)
    def _():
        stage_core(value_ref)

    @pl.when(core == 1)
    def _():
        stage_core(key_ref)

    first = send(staged.at[pl.ds(0, rows)], landed.at[pl.ds(0, rows)], 0, partner_of(position, ("tm", 0)))
    first.wait()

    def add_core(ref):
        def body(at, _, __):
            held[at, :] = ref[at, :] + landed[at, :].astype(jnp.float32)

        each(0, rows, body)

    @pl.when(core == 0)
    def _():
        add_core(key_ref)

    @pl.when(core == 1)
    def _():
        add_core(value_ref)

    steps = len(orders[0])
    begin = [jnp.int32(0) for _ in orders]
    size = rows
    base = rows
    starts = [list(begin)]
    for step in range(steps):
        size //= 2
        copies = []
        for p, order in enumerate(orders):
            axis, k = order[step]
            bit = bit_of(position[axis], k)
            cols = pl.ds(edges[p], edges[p + 1] - edges[p])
            away = begin[p] + (1 - bit) * size
            begin[p] = begin[p] + bit * size

            def body(at, i, piece, cols=cols):
                staged[pl.ds(pl.multiple_of(base + i, piece), piece), cols] = held[at, cols].astype(
                    staged.dtype
                )

            each(away, size, body)
            copies.append(
                send(
                    staged.at[pl.ds(base, size), cols],
                    landed.at[pl.ds(base, size), cols],
                    1 + step * 3 + p,
                    partner_of(position, order[step]),
                )
            )
        for p, copy in enumerate(copies):
            copy.wait()
            cols = pl.ds(edges[p], edges[p + 1] - edges[p])

            def body(at, i, piece, cols=cols):
                held[at, cols] += landed[pl.ds(pl.multiple_of(base + i, piece), piece), cols].astype(
                    jnp.float32
                )

            each(begin[p], size, body)
        starts.append(list(begin))
        base += size

    for p in range(3):
        cols = pl.ds(edges[p], edges[p + 1] - edges[p])

        def body(at, i, piece, cols=cols, p=p):
            out_ref[
                pl.ds(pl.multiple_of(core * rows + begin[p] + i, piece), piece), cols
            ] = held[at, cols].astype(out_ref.dtype)

        each(begin[p], size, body)

    slot = 1 + steps * 3
    for step in range(steps - 1, -1, -1):
        copies = []
        for p, order in enumerate(orders):
            at = (
                pl.ds(pl.multiple_of(core * rows + starts[step + 1][p], size), size),
                pl.ds(edges[p], edges[p + 1] - edges[p]),
            )
            copies.append(
                send(out_ref.at[at], out_ref.at[at], slot + step * 3 + p, partner_of(position, order[step]))
            )
        for copy in copies:
            copy.wait()
        size *= 2
    at = pl.ds(pl.multiple_of(core * rows, rows), rows)
    send(out_ref.at[at], out_ref.at[at], slot + steps * 3, partner_of(position, ("tm", 0))).wait()


def sum_everywhere(key_term, value_term, bits):
    rows, width = key_term.shape
    slots = 2 + 6 * (bits[0] + bits[1] - 1)
    return pl.pallas_call(
        functools.partial(sum_kernel, bits),
        out_shape=jax.ShapeDtypeStruct((2 * rows, width), jnp.bfloat16),
        in_specs=[pl.BlockSpec(memory_space=pltpu.VMEM)] * 2,
        out_specs=pl.BlockSpec(memory_space=pltpu.VMEM),
        scratch_shapes=[
            pltpu.VMEM((rows, width), jnp.float32),
            pltpu.VMEM((2 * rows, width), jnp.bfloat16),
            pltpu.VMEM((2 * rows, width), jnp.bfloat16),
            pltpu.SemaphoreType.DMA((slots,)),
            pltpu.SemaphoreType.DMA((slots,)),
        ],
        compiler_params=pltpu.CompilerParams(
            collective_id=1, has_side_effects=True, vmem_limit_bytes=48 << 20
        ),
    )(key_term, value_term)


def attend(queries, keys, values, lengths, cotangent, seqs):
    score_scale = 1.0 / math.sqrt(queries.shape[-1])
    steps = queries.shape[0] // seqs
    dot = functools.partial(lax.dot_general, preferred_element_type=jnp.float32)
    rows_rows = (((1,), (1,)), ((), ()))
    rows_cols = (((1,), (0,)), ((), ()))
    cols_cols = (((0,), (0,)), ((), ()))
    scores = dot(queries, keys, rows_rows) * score_scale
    row = lax.broadcasted_iota(jnp.int32, (queries.shape[0], 1), 0) // steps
    column = lax.broadcasted_iota(jnp.int32, (1, keys.shape[0]), 1)
    limit = jnp.repeat(lengths, steps)[:, None]
    seen = (column % seqs == row) & (column // seqs < limit)
    scores = jnp.where(seen, scores, -1e30)
    row_max = jnp.max(scores, axis=-1, keepdims=True)
    weights = jnp.where(seen, jnp.exp(scores - row_max), 0.0)
    probabilities = weights / jnp.sum(weights, axis=-1, keepdims=True)
    probs_low = probabilities.astype(jnp.bfloat16)
    context = dot(probs_low, values, rows_cols).astype(jnp.bfloat16)
    grad_probs = dot(cotangent, values, rows_rows)
    grad_scores = probabilities * (
        grad_probs - jnp.sum(probabilities * grad_probs, axis=-1, keepdims=True)
    )
    grad_low = grad_scores.astype(jnp.bfloat16)
    grad_values = dot(probs_low, cotangent, cols_cols).astype(jnp.bfloat16)
    grad_keys = (dot(grad_low, queries, cols_cols) * score_scale).astype(jnp.bfloat16)
    return context, grad_keys, grad_values


def project(flattened, weight_matrix):
    return jnp.dot(flattened, weight_matrix, preferred_element_type=jnp.float32).astype(jnp.bfloat16)


def weight_term(flattened, gradient):
    return lax.dot_general(
        flattened, gradient, (((0,), (0,)), ((), ())), preferred_element_type=jnp.float32
    )


def body(n_tm, n_dp, encoded, queries, cotangent, lengths, key_weight, value_weight):
    width = encoded.shape[2]
    seqs = queries.shape[0]
    flattened = exchange(encoded, n_tm).reshape(-1, width)
    key_rows = project(flattened, key_weight)
    value_rows = project(flattened, value_weight)
    context, grad_keys, grad_values = attend(
        queries.reshape(-1, width), key_rows, value_rows, lengths, cotangent.reshape(-1, width), seqs
    )
    key_term = weight_term(flattened, grad_keys)
    value_term = weight_term(flattened, grad_values)
    sums = sum_everywhere(
        key_term, value_term, (n_tm.bit_length() - 1, n_dp.bit_length() - 1)
    ).astype(jnp.float32)
    return context.reshape(queries.shape), sums[: key_term.shape[0]], sums[key_term.shape[0] :]


def solution(mesh):
    return jax.shard_map(
        functools.partial(body, mesh.shape["tm"], mesh.shape["dp"]),
        mesh=mesh,
        in_specs=(
            P("dp", "tm", None),
            P(("dp", "tm"), None, None),
            P(("dp", "tm"), None, None),
            P(("dp", "tm")),
            P(),
            P(),
        ),
        out_specs=(P(("dp", "tm"), None, None), P(), P()),
        check_vma=False,
    )
```

time: 356 us -> 181 us (0.51)
  waiting for transfers between devices: 268 us -> 0 us
  Pallas kernels: 0 us -> 129 us
  local copies, waits for them, and re-layouts: 27.4 us -> 8.88 us
  between operations: 14.1 us -> 0.68 us
  starting transfers between devices: 6.52 us -> 0 us
    psum x1 -> x0, waiting for transfers between devices: 174 us -> none  [body(): key_grad, value_grad = lax.psum((key_grad, value_grad), ('tm', 'dp'))]
    pallas_call x0 -> x2, Pallas kernels: none -> 129 us  [the longest x1 66.7 us: sum_everywhere(): pl.pallas_call(functools.partial(sum_kernel, bits), out_shape=jax.ShapeDt...]
    all_to_all x1 -> x0, waiting for transfers between devices: 94 us -> none  [body(): lax.all_to_all(encoded, 'tm', split_axis=0, concat_axis=1, tiled=True)]
    unnamed x17 -> x14, local copies, waits for them, and re-layouts: 16.2 us -> 3.46 us
    dot_general x7 -> x5, matrix products: 29 us -> 35.8 us  [the longest x2 19.4 us: weight_term(): lax.dot_general(flattened, gradient, (((0,), (0,)), ((), ())), preferred_...]
    all_to_all x1 -> x0, starting transfers between devices: 6.49 us -> none  [body(): lax.all_to_all(encoded, 'tm', split_axis=0, concat_axis=1, tiled=True)]
    reshape x1 -> x0, local copies, waits for them, and re-layouts: 6.14 us -> none  [body(): flattened = regrouped.reshape(-1, model_width)]
    dot_general x2 -> x1, matrix products: 9.23 us -> 4.13 us  [project(): jnp.dot(flattened, weight_matrix, preferred_element_type=jnp.float32)]
  transfers between devices with their start and end apart: 2 -> 0, of which waited for: 2 -> 0; matrix products, arithmetic and copies ran while one was open for 1% -> 0% of each run, Pallas kernels for 0% -> 0%
where the time goes in v1:
time: 181 us
  Pallas kernels  129 us (71%)
  matrix products  39.9 us (22%)
  local copies, waits for them, and re-layouts  8.88 us (5%)
  other arithmetic  2.33 us (1%)
    pallas_call x1, Pallas kernels, sum_everywhere(): pl.pallas_call(functools.partial(sum_kernel, bits), out_shape=jax.ShapeDt...  66.7 us
    pallas_call x1, Pallas kernels, exchange(): pl.pallas_call(functools.partial(exchange_kernel, n), out_shape=jax.Shape...  62.8 us
    dot_general x2, matrix products, weight_term(): lax.dot_general(flattened, gradient, (((0,), (0,)), ((), ())), preferred_...  19.4 us
    dot_general x1, matrix products, attend(): scores = dot(queries, keys, rows_rows) * score_scale  8.38 us
    dot_general x1, matrix products, attend(): context = dot(probs_low, values, rows_cols).astype(jnp.bfloat16)  4.66 us
    slice x1, local copies, waits for them, and re-layouts, body(): sums[key_term.shape[0]:]  4.46 us
    dot_general x1, matrix products, project(): jnp.dot(flattened, weight_matrix, preferred_element_type=jnp.float32)  4.13 us

profile of v1, /device:TPU:0, one launch (start us, length us, event | category | flops | bytes accessed | tf_op | source)
XLA Modules:
  0.0 181.3 jit_solution(8316857266660716949)
XLA Ops:
  0.6 0.0 copy-start
  0.7 0.9 broadcast_in_dim.13
  1.5 0.1 lt.23
  1.6 0.0 copy-start.1
  1.6 1.7 copy-done.1
  3.4 62.8 %shard_map.85 = bf16[8,10,16,1024]{3,2,1,0:T(8,128)(2,1)S(1)} custom-call(bf16[10,128,1024]{2,1,0:T(8,128)(2,1)S(1)} %bitcast.27), custom_call_target="tpu_custom_call" | custom-call | tf_op jit(solution)/shard_map/pallas_call | solution.py:63
  66.2 0.0 copy-start.2
  66.2 1.5 copy-done.2
  67.7 0.0 copy-done
  67.7 0.0 copy-start.4
  67.7 4.1 %convolution_convert_fusion.1 = bf16[1280,1024]{1,0:T(8,128)(2,1)} fusion(bf16[1280,1024]{1,0:T(8,128)(2,1)S(1)} %bitcast.28, bf16[1024,1024]{1,0:T(8,128)(2,1)S(1)} %copy-done), kind=kOutput, calls=%fused_computation.2 | convolution fusion | flops 2685665280 | bytes 7340032 | tf_op jit(solution)/shard_map/dot_general | solution.py:273
  71.8 0.0 copy-done.4
  71.8 8.4 %fusion.23 = (f32[512]{0:T(512)S(1)}, f32[512,1280]{0,1:T(8,128)}) fusion(bf16[512,1024]{1,0:T(8,128)(2,1)S(1)} %bitcast.32, bf16[1280,1024]{1,0:T(8,128)(2,1)} %bitcast.29, bf16[1024,1024]{1,0:T(8,128)(2,1)} %param.10, s32[512]{0:T(512)S(1)} %lt.23, s32[1280]{0:T(1024)S(1)} %get-tuple-element.9, s32[512]{0:T(512)S(1)} %add_select_fusion.2, ...), kind=kOutput, calls=%fused_computation.39 | convolution fusion | flops 4031774208 | bytes 8404992 | tf_op jit(solution)/shard_map/dot_general | solution.py:251
  80.2 0.0 copy-start.3
  80.2 2.3 %fusion.3 = f32[512]{0:T(512)S(1)} fusion(f32[512,1280]{0,1:T(8,128)} %get-tuple-element.6, f32[512]{0:T(512)S(1)} %get-tuple-element.5, s32[512]{0:T(512)S(1)} %lt.23, s32[512]{0:T(512)S(1)} %add_select_fusion.2, s32[1280]{0:T(1024)S(1)} %get-tuple-element.9, s32[1280]{0:T(1024)S(1)} %get-tuple-element.10), kind=kLoop, calls=%fused_computation.15 | loop fusion | flops 3931648 | bytes 2639872 | tf_op jit(solution)/shard_map/reduce_sum | solution.py:259
  82.5 0.2 copy-done.3
  82.8 4.7 %convolution_convert_fusion.3 = bf16[512,1024]{1,0:T(8,128)(2,1)} fusion(bf16[1280,1024]{1,0:T(8,128)(2,1)} %convolution_convert_fusion.1, f32[512,1280]{0,1:T(8,128)S(1)} %copy-done.3, f32[512]{0:T(512)S(1)} %fusion.3, f32[512]{0:T(512)S(1)} %get-tuple-element.5, s32[512]{0:T(512)S(1)} %lt.23, s32[512]{0:T(512)S(1)} %add_select_fusion.2, ...), kind=kOutput, calls=%fused_computation.16 | convolution fusion | flops 1347289088 | bytes 6309888 | tf_op jit(solution)/shard_map/dot_general | solution.py:261
  87.4 0.0 copy-done.5
  87.4 0.0 copy-done.6
  87.4 3.4 %multiply_reduce_fusion = (f32[512]{0:T(512)S(1)}, f32[512,1280]{0,1:T(8,128)}) fusion(f32[512]{0:T(512)S(1)} %fusion.3, f32[512,1280]{0,1:T(8,128)S(1)} %copy-done.3, f32[512]{0:T(512)S(1)} %get-tuple-element.5, s32[512]{0:T(512)S(1)} %lt.23, s32[1280]{0:T(1024)S(1)} %get-tuple-element.9, s32[512]{0:T(512)S(1)} %add_select_fusion.2, ...), kind=kOutput, calls=%fused_computation.9 | convolution fusion | flops 1347419648 | bytes 8933376 | tf_op jit(solution)/shard_map/dot_general | solution.py:262
  90.8 10.0 %convolution_bitcast_fusion.2.key_ref = f32[1024,1024]{1,0:T(8,128)} fusion(bf16[1280,1024]{1,0:T(8,128)(2,1)} %bitcast.30, bf16[512,1024]{1,0:T(8,128)(2,1)S(1)} %bitcast.33, f32[512,1280]{0,1:T(8,128)} %get-tuple-element.8, f32[512]{0:T(512)S(1)} %get-tuple-element.7, f32[512,1280]{0,1:T(8,128)} %get-tuple-element.6, f32[512]{0:T(512)S(1)} %fusion.3, ...), kind=kOutput, calls=%fused_computation.13 | convolution fusion | flops 4035051520 | bytes 13127680 | tf_op jit(solution)/shard_map/dot_general | solution.py:277
  100.8 9.4 %convolution_bitcast_fusion.1.value_ref = f32[1024,1024]{1,0:T(8,128)} fusion(bf16[1280,1024]{1,0:T(8,128)(2,1)} %bitcast.31, bf16[512,1024]{1,0:T(8,128)(2,1)} %bitcast.34, f32[512,1280]{0,1:T(8,128)} %get-tuple-element.6, f32[512]{0:T(512)S(1)} %fusion.3, f32[512]{0:T(512)S(1)} %get-tuple-element.5, s32[512]{0:T(512)S(1)} %lt.23, ...), kind=kOutput, calls=%fused_computation.12 | convolution fusion | flops 4032430080 | bytes 10504192 | tf_op jit(solution)/shard_map/dot_general | solution.py:277
  110.2 66.7 %shard_map.86 = bf16[2048,1024]{1,0:T(8,128)(2,1)S(1)} custom-call(f32[1024,1024]{1,0:T(8,128)} %convolution_bitcast_fusion.2.key_ref, f32[1024,1024]{1,0:T(8,128)} %convolution_bitcast_fusion.1.value_ref), custom_call_target="tpu_custom_call" | custom-call | tf_op jit(solution)/shard_map/pallas_call | solution.py:226
  176.8 4.5 %fusion.22 = (f32[1024,1024]{1,0:T(8,128)}, f32[1024,1024]{1,0:T(8,128)}) fusion(bf16[2048,1024]{1,0:T(8,128)(2,1)S(1)} %shard_map.86), kind=kLoop, calls=%fused_computation.38 | loop fusion | bytes 16777216 | tf_op jit(solution)/shard_map/slice | solution.py:296
  (4 shorter events, 0.0 us)
Async XLA Ops:
  0.6 67.1 %copy-start = (bf16[1024,1024]{1,0:T(8,128)(2,1)S(1)}, bf16[1024,1024]{1,0:T(8,128)(2,1)}, u32[]{:S(2)}) copy-start(bf16[1024,1024]{1,0:T(8,128)(2,1)} %param.11) | copy-start | bytes 6291460
  1.6 1.7 copy-start.1
  66.2 1.5 copy-start.2
  67.7 4.1 %copy-start.4 = (bf16[16,32,1024]{2,1,0:T(8,128)(2,1)S(1)}, bf16[16,32,1024]{2,1,0:T(8,128)(2,1)}, u32[]{:S(2)}) copy-start(bf16[16,32,1024]{2,1,0:T(8,128)(2,1)} %param.7) | copy-start | bytes 3145732
  80.2 2.5 %copy-start.3 = (f32[512,1280]{0,1:T(8,128)S(1)}, f32[512,1280]{0,1:T(8,128)}, u32[]{:S(2)}) copy-start(f32[512,1280]{0,1:T(8,128)} %get-tuple-element.6) | copy-start | bytes 7864324
  82.7 4.7 %copy-start.5 = (bf16[16,32,1024]{2,1,0:T(8,128)(2,1)S(1)}, bf16[16,32,1024]{2,1,0:T(8,128)(2,1)}, u32[]{:S(2)}) copy-start(bf16[16,32,1024]{2,1,0:T(8,128)(2,1)} %param.8) | copy-start | bytes 3145732
  82.8 4.7 %copy-start.6 = (bf16[1280,1024]{1,0:T(8,128)(2,1)S(1)}, bf16[1280,1024]{1,0:T(8,128)(2,1)}, u32[]{:S(2)}) copy-start(bf16[1280,1024]{1,0:T(8,128)(2,1)} %convolution_convert_fusion.1) | copy-start | bytes 7864324

commit v2 on v1

--- a/solution.py
+++ b/solution.py
@@ -31,14 +31,14 @@
     pl.semaphore_wait(barrier, len(devices))
 
 
-def exchange_kernel(n, enc_ref, out_ref, send_sem, recv_sem, own_sem):
+def exchange_kernel(n, enc_ref, kw_ref, vw_ref, out_ref, key_ref, value_ref, send_sem, recv_sem, own_sem):
     me = lax.axis_index("tm")
-    seqs = out_ref.shape[2]
+    _, positions, seqs, width = out_ref.shape
     greet([{"tm": flip(me, d)} for d in range(1, n)])
-    copies = []
+    copies = {}
     for d in range(n - 1, 0, -1):
         target = flip(me, d)
-        copy = pltpu.make_async_remote_copy(
+        copies[d] = pltpu.make_async_remote_copy(
             src_ref=enc_ref.at[:, pl.ds(pl.multiple_of(target * seqs, seqs), seqs), :],
             dst_ref=out_ref.at[me],
             send_sem=send_sem.at[d],
@@ -46,34 +46,50 @@
             device_id={"tm": target},
             device_id_type=MESH,
         )
-        copy.start()
-        copies.append(copy)
+        copies[d].start()
     own = pltpu.make_async_copy(
         enc_ref.at[:, pl.ds(pl.multiple_of(me * seqs, seqs), seqs), :], out_ref.at[me], own_sem
     )
     own.start()
     own.wait()
-    for copy in copies:
-        copy.wait()
-
-
-def exchange(encoded, n):
+
+    def project(source):
+        block = out_ref[source].reshape(positions * seqs, width)
+        for weight, rows in ((kw_ref, key_ref), (vw_ref, value_ref)):
+            rows[source] = jnp.dot(
+                block, weight[...], preferred_element_type=jnp.float32
+            ).astype(rows.dtype)
+
+    project(me)
+    for d in [1] + list(range(n - 1, 1, -1)):
+        copies[d].wait()
+        project(flip(me, d))
+
+
+def exchange(encoded, key_weight, value_weight, n):
     by_position = jnp.swapaxes(encoded, 0, 1)
     positions, rows, width = by_position.shape
-    return pl.pallas_call(
+    taken = (n, positions, rows // n, width)
+    projected = (n, positions * rows // n, width)
+    results = pl.pallas_call(
         functools.partial(exchange_kernel, n),
-        out_shape=jax.ShapeDtypeStruct((n, positions, rows // n, width), encoded.dtype),
-        in_specs=[pl.BlockSpec(memory_space=pltpu.VMEM)],
-        out_specs=pl.BlockSpec(memory_space=pltpu.VMEM),
+        out_shape=[
+            jax.ShapeDtypeStruct(taken, encoded.dtype),
+            jax.ShapeDtypeStruct(projected, encoded.dtype),
+            jax.ShapeDtypeStruct(projected, encoded.dtype),
+        ],
+        in_specs=[pl.BlockSpec(memory_space=pltpu.VMEM)] * 3,
+        out_specs=[pl.BlockSpec(memory_space=pltpu.VMEM)] * 3,
         scratch_shapes=[
             pltpu.SemaphoreType.DMA((n,)),
             pltpu.SemaphoreType.DMA((n,)),
             pltpu.SemaphoreType.DMA,
         ],
         compiler_params=pltpu.CompilerParams(
-            collective_id=0, has_side_effects=True, vmem_limit_bytes=40 << 20
+            collective_id=0, has_side_effects=True, vmem_limit_bytes=48 << 20
         ),
-    )(by_position)
+    )(by_position, key_weight, value_weight)
+    return [result.reshape(-1, width) for result in results]
 
 
 def orders_of(bits_tm, bits_dp):
@@ -269,10 +285,6 @@
     return context, grad_keys, grad_values
 
 
-def project(flattened, weight_matrix):
-    return jnp.dot(flattened, weight_matrix, preferred_element_type=jnp.float32).astype(jnp.bfloat16)
-
-
 def weight_term(flattened, gradient):
     return lax.dot_general(
         flattened, gradient, (((0,), (0,)), ((), ())), preferred_element_type=jnp.float32
@@ -282,9 +294,7 @@
 def body(n_tm, n_dp, encoded, queries, cotangent, lengths, key_weight, value_weight):
     width = encoded.shape[2]
     seqs = queries.shape[0]
-    flattened = exchange(encoded, n_tm).reshape(-1, width)
-    key_rows = project(flattened, key_weight)
-    value_rows = project(flattened, value_weight)
+    flattened, key_rows, value_rows = exchange(encoded, key_weight, value_weight, n_tm)
     context, grad_keys, grad_values = attend(
         queries.reshape(-1, width), key_rows, value_rows, lengths, cotangent.reshape(-1, width), seqs
     )

time: 181 us -> 178 us (0.983)
  matrix products: 39.9 us -> 28.6 us
  Pallas kernels: 129 us -> 136 us
  local copies, waits for them, and re-layouts: 8.88 us -> 11.4 us
    pallas_call x1, Pallas kernels: 62.8 us -> 69.4 us  [exchange(): pl.pallas_call(functools.partial(exchange_kernel, n), out_shape=[jax.Shap...]
    dot_general x1, matrix products: 8.38 us -> 3.37 us  [attend(): scores = dot(queries, keys, rows_rows) * score_scale]
    dot_general x1 -> x0, matrix products: 4.13 us -> none  [project(): jnp.dot(flattened, weight_matrix, preferred_element_type=jnp.float32)]
    unnamed x14 -> x12, local copies, waits for them, and re-layouts: 3.46 us -> 6.11 us
    dot_general x1, matrix products: 4.66 us -> 2.76 us  [attend(): context = dot(probs_low, values, rows_cols).astype(jnp.bfloat16)]
where the time goes in v2:
time: 178 us
  Pallas kernels  136 us (76%)
  matrix products  28.6 us (16%)
  local copies, waits for them, and re-layouts  11.4 us (6%)
    pallas_call x1, Pallas kernels, exchange(): pl.pallas_call(functools.partial(exchange_kernel, n), out_shape=[jax.Shap...  69.4 us
    pallas_call x1, Pallas kernels, sum_everywhere(): pl.pallas_call(functools.partial(sum_kernel, bits), out_shape=jax.ShapeDt...  66.6 us
    dot_general x2, matrix products, weight_term(): lax.dot_general(flattened, gradient, (((0,), (0,)), ((), ())), preferred_...  19 us
    unnamed x12, local copies, waits for them, and re-layouts  6.11 us
    slice x1, local copies, waits for them, and re-layouts, body(): sums[key_term.shape[0]:]  4.44 us

profile of v2, /device:TPU:0, one launch (start us, length us, event | category | flops | bytes accessed | tf_op | source)
XLA Modules:
  0.0 177.6 jit_solution(64874411326580310)
XLA Ops:
  0.6 0.0 copy-start
  0.6 1.2 copy-done
  1.9 0.7 broadcast_in_dim.13
  2.6 0.1 lt.23
  2.7 0.0 copy-start.1
  2.7 1.6 copy-done.1
  4.3 0.0 copy-start.2
  4.3 1.6 copy-done.2
  5.9 69.4 %shard_map.85 = (bf16[8,10,16,1024]{3,2,1,0:T(8,128)(2,1)}, bf16[8,160,1024]{2,1,0:T(8,128)(2,1)}, bf16[8,160,1024]{2,1,0:T(8,128)(2,1)}) custom-call(bf16[10,128,1024]{2,1,0:T(8,128)(2,1)} %bitcast.24, bf16[1024,1024]{1,0:T(8,128)(2,1)S(1)} %copy-done.1, bf16[1024,1024]{1,0:T(8,128)(2,1)S(1)} %copy-done.2), custom_call_target="tpu_custom_call" | custom-call | tf_op jit(solution)/shard_map/pallas_call | solution.py:74
  75.3 3.4 %fusion.25 = (f32[512]{0:T(512)S(1)}, f32[512,1280]{0,1:T(8,128)S(1)}) fusion(bf16[1280,1024]{1,0:T(8,128)(2,1)} %bitcast.29, bf16[512,1024]{1,0:T(8,128)(2,1)S(1)} %bitcast.22, s32[512]{0:T(512)S(1)} %lt.23, s32[1280]{0:T(1024)S(1)} %get-tuple-element.15, s32[512]{0:T(512)S(1)} %add_select_fusion.2, s32[1280]{0:T(1024)S(1)} %get-tuple-element.16), kind=kOutput, calls=%fused_computation.37 | convolution fusion | flops 1346108928 | bytes 6307840 | tf_op jit(solution)/shard_map/dot_general | solution.py:267
  78.6 0.0 copy-start.3
  78.6 0.0 copy-start.4
  78.6 1.0 fusion.3
  79.6 1.7 copy-done.4
  81.3 0.0 copy-start.5
  81.3 2.8 %convolution_convert_fusion.1 = bf16[512,1024]{1,0:T(8,128)(2,1)} fusion(bf16[1280,1024]{1,0:T(8,128)(2,1)S(1)} %bitcast.27, f32[512,1280]{0,1:T(8,128)S(1)} %get-tuple-element.12, f32[512]{0:T(512)S(1)} %fusion.3, f32[512]{0:T(512)S(1)} %get-tuple-element.11, s32[512]{0:T(512)S(1)} %lt.23, s32[512]{0:T(512)S(1)} %add_select_fusion.2, ...), kind=kOutput, calls=%fused_computation.12 | convolution fusion | flops 1347289088 | bytes 6309888 | tf_op jit(solution)/shard_map/dot_general | solution.py:277
  84.1 0.0 copy-done.3
  84.1 0.0 copy-done.5
  84.1 3.4 %multiply_reduce_fusion = (f32[512]{0:T(512)S(1)}, f32[512,1280]{0,1:T(8,128)}) fusion(f32[512]{0:T(512)S(1)} %fusion.3, f32[512,1280]{0,1:T(8,128)S(1)} %get-tuple-element.12, f32[512]{0:T(512)S(1)} %get-tuple-element.11, s32[512]{0:T(512)S(1)} %lt.23, s32[1280]{0:T(1024)S(1)} %get-tuple-element.15, s32[512]{0:T(512)S(1)} %add_select_fusion.2, ...), kind=kOutput, calls=%fused_computation.7 | convolution fusion | flops 1347419648 | bytes 8933376 | tf_op jit(solution)/shard_map/dot_general | solution.py:278
  87.5 10.0 %fusion.6.key_ref = f32[1024,1024]{1,0:T(8,128)} fusion(bf16[1280,1024]{1,0:T(8,128)(2,1)} %bitcast.25, bf16[512,1024]{1,0:T(8,128)(2,1)S(1)} %bitcast.23, f32[512,1280]{0,1:T(8,128)} %get-tuple-element.14, f32[512]{0:T(512)S(1)} %get-tuple-element.13, f32[512,1280]{0,1:T(8,128)} %copy-done.3, f32[512]{0:T(512)S(1)} %fusion.3, ...), kind=kOutput, calls=%fused_computation.15 | convolution fusion | flops 4035051520 | bytes 13127680 | tf_op jit(solution)/shard_map/dot_general | solution.py:289
  97.5 9.1 %fusion.5.value_ref = f32[1024,1024]{1,0:T(8,128)} fusion(bf16[1280,1024]{1,0:T(8,128)(2,1)} %bitcast.26, bf16[512,1024]{1,0:T(8,128)(2,1)S(1)} %bitcast.31, f32[512,1280]{0,1:T(8,128)} %copy-done.3, f32[512]{0:T(512)S(1)} %fusion.3, f32[512]{0:T(512)S(1)} %get-tuple-element.11, s32[512]{0:T(512)S(1)} %lt.23, s32[512]{0:T(512)S(1)} %add_select_fusion.2, ...), kind=kOutput, calls=%fused_computation.14 | convolution fusion | flops 4032430080 | bytes 10504192 | tf_op jit(solution)/shard_map/dot_general | solution.py:289
  106.5 66.6 %shard_map.86 = bf16[2048,1024]{1,0:T(8,128)(2,1)S(1)} custom-call(f32[1024,1024]{1,0:T(8,128)} %fusion.6.key_ref, f32[1024,1024]{1,0:T(8,128)} %fusion.5.value_ref), custom_call_target="tpu_custom_call" | custom-call | tf_op jit(solution)/shard_map/pallas_call | solution.py:242
  173.1 4.4 %fusion.24 = (f32[1024,1024]{1,0:T(8,128)}, f32[1024,1024]{1,0:T(8,128)}) fusion(bf16[2048,1024]{1,0:T(8,128)(2,1)S(1)} %shard_map.86), kind=kLoop, calls=%fused_computation.36 | loop fusion | bytes 16777216 | tf_op jit(solution)/shard_map/slice | solution.py:306
  (2 shorter events, 0.0 us)
Async XLA Ops:
  0.6 1.2 copy-start
  2.7 1.6 copy-start.1
  4.3 1.6 copy-start.2
  78.6 5.5 %copy-start.3 = (f32[512,1280]{0,1:T(8,128)}, f32[512,1280]{0,1:T(8,128)S(1)}, u32[]{:S(2)}) copy-start(f32[512,1280]{0,1:T(8,128)S(1)} %get-tuple-element.12) | copy-start | bytes 7864324
  78.6 2.7 %copy-start.4 = (bf16[8,160,1024]{2,1,0:T(8,128)(2,1)S(1)}, bf16[8,160,1024]{2,1,0:T(8,128)(2,1)}, u32[]{:S(2)}) copy-start(bf16[8,160,1024]{2,1,0:T(8,128)(2,1)} %get-tuple-element.7) | copy-start | bytes 7864324
  81.3 2.8 %copy-start.5 = (bf16[16,32,1024]{2,1,0:T(8,128)(2,1)S(1)}, bf16[16,32,1024]{2,1,0:T(8,128)(2,1)}, u32[]{:S(2)}) copy-start(bf16[16,32,1024]{2,1,0:T(8,128)(2,1)} %param.8) | copy-start | bytes 3145732
